TPU v7x, 128 devices: a 2x2x16 block of a 8x8x16 slice. The times are simulated.
128 devices in a mesh: grp: 4 (over y, x), seq: 32 (over z, core).
Axes of the slice: x: 2, y: 2, z: 16, core: 2. Of those that a mesh axis runs over, the one named last changes fastest.
The devices are a block of a 8x8x16 slice.
Arguments:
- queries: bfloat16 [2048, 4096], P(('grp', 'seq')), parts along dimension 0, may hold values from -36 to 36
- new_keys: bfloat16 [2048, 1024], P(('grp', 'seq')), parts along dimension 0, may hold values from -24 to 24
- new_values: bfloat16 [2048, 1024], P(('grp', 'seq')), parts along dimension 0, may hold values from -12 to 12
- suffix_keys: bfloat16 [2048, 256, 1024], P(('grp', 'seq')), parts along dimension 0, may hold values from -18 to 18
- suffix_values: bfloat16 [2048, 256, 1024], P(('grp', 'seq')), parts along dimension 0, may hold values from -12 to 12
- suffix_lens: int32 [2048], P(('grp', 'seq')), parts along dimension 0, may hold values from 1 to 256, 65536 in all
- prefix_keys: bfloat16 [8192, 16, 1024], P(('grp', 'seq')), parts along dimension 0, may hold values from -12 to 12
- prefix_values: bfloat16 [8192, 16, 1024], P(('grp', 'seq')), parts along dimension 0, may hold values from -12 to 12
- page_table: int32 [8, 1024], P('grp'), parts along dimension 0, may hold values from 0 to 2047, as said below
- prefix_id: int32 [2048], P('grp'), parts along dimension 0, may hold values from 0 to 1
Outputs:
- attn_out: bfloat16 [2048, 4096], P(('grp', 'seq')), parts along dimension 0
There are 4 independent parts, one for each index of `grp`. A program takes and returns all parts, laid end to end along the dimension named above; each array names one. Nothing has to cross between parts.
Inputs may be any that keep to these rules, and one draw needn't show every extreme that they name: `page_table`: every page id 0 to 2047 stands exactly once in the table. Each run of 64 page ids that starts at a multiple of 64 holds at least one page of every prefix.
All inputs are finite; a program needn't handle non-finite values. No bound on the sum of `suffix_lens` on one device may be relied on, other than what follows from the above.
Results may differ from a plain program's by a relative error of at most 0.005.
Values may be sent and summed in bfloat16 or wider, within the bound.
A program may use at most 192 MiB of HBM per device.

v0:
```python
import math

import jax
import jax.numpy as jnp
from jax import lax
from jax.sharding import Mesh
from jax.sharding import PartitionSpec as P

H = 32
KV = 8
HD = 128
NPREF = 2
SEQ = ("seq_0", "seq_1")
GRP_SEQ = ("grp", "seq_0", "seq_1")


floor_score = -1e30


def split_up(array, dim, peers):
    before, after = (array.shape[:dim], array.shape[dim + 1 :])
    return jnp.moveaxis(array.reshape(*before, peers, -1, *after), dim, 0)


def laid_out(tiles, dim):
    tiles = jnp.moveaxis(tiles, 0, dim)
    lengths = tiles.shape
    return tiles.reshape(*lengths[:dim], lengths[dim] * lengths[dim + 1], *lengths[dim + 2 :])


def moved_by_axis(tiles, axes, sequence):
    lengths = [lax.axis_size(a) for a in axes]
    tiles = tiles.reshape(*lengths, *tiles.shape[1:])
    for k in sequence:
        tiles = lax.all_to_all(tiles, axes[k], split_axis=k, concat_axis=k, tiled=True)
    return tiles.reshape(-1, *tiles.shape[len(axes) :])


def two_step_exchange(array, groups, sequence, split_dim, concat_dim):
    peers = lax.axis_size(groups[0]) * lax.axis_size(groups[1])
    tiles = split_up(array, split_dim, peers)
    return laid_out(moved_by_axis(tiles, groups, sequence), concat_dim)


def local(
    queries,
    new_keys,
    new_values,
    suffix_keys,
    suffix_values,
    suffix_lens,
    prefix_keys,
    prefix_values,
    page_table,
    prefix_id,
):
    local_rows = queries.shape[0]
    group_size = H // KV
    softmax_scale = 1.0 / math.sqrt(HD)
    owner_count = lax.axis_size(SEQ)
    owner_index = lax.axis_index(SEQ)
    pages_dev = prefix_keys.shape[0]
    local_ids = owner_index * pages_dev + jnp.arange(pages_dev, dtype=jnp.int32)
    page_hits = jnp.any(page_table[:, :, None] == local_ids[None, None, :], axis=1)
    page_label = jnp.sum(
        page_hits.astype(jnp.int32) * jnp.arange(NPREF, dtype=jnp.int32)[:, None], axis=0
    )
    token_label = jnp.repeat(page_label, prefix_keys.shape[1])
    keys_local = prefix_keys.reshape(-1, KV, HD)
    values_local = prefix_values.reshape(-1, KV, HD)
    shard_rows = lax.all_gather(queries, SEQ, axis=0, tiled=True)
    piece_rows = shard_rows.shape[0]
    query_head_count = shard_rows.reshape(piece_rows, KV, group_size, HD)
    scores = (
        jnp.einsum(
            "bkgd,tkd->bkgt", query_head_count, keys_local, preferred_element_type=jnp.float32
        )
        * softmax_scale
    )
    allowed = (prefix_id[:, None] == token_label[None, :])[:, None, None, :]
    scores = jnp.where(allowed, scores, floor_score)
    row_peak = jnp.max(scores, axis=3)
    weights = jnp.where(allowed, jnp.exp(scores - row_peak[..., None]), 0.0)
    weight_sum = jnp.sum(weights, axis=3)
    numerator = jnp.einsum(
        "bkgt,tkd->bkgd",
        weights.astype(jnp.bfloat16),
        values_local,
        preferred_element_type=jnp.float32,
    )
    piece_out = (numerator / weight_sum[..., None]).astype(jnp.bfloat16).reshape(piece_rows, -1)
    piece_lse = (row_peak + jnp.log(weight_sum)).reshape(-1)
    out_all = piece_out
    lse_all = piece_lse
    out_all, lse_all = (out_all, lse_all)
    resident_heads = queries.reshape(local_rows, KV, group_size, HD)
    slot_count = suffix_keys.shape[1]
    own_keys = suffix_keys.reshape(local_rows, slot_count, KV, HD)
    own_values = suffix_values.reshape(local_rows, slot_count, KV, HD)
    suffix_scores = (
        jnp.einsum("bkgd,btkd->bkgt", resident_heads, own_keys, preferred_element_type=jnp.float32)
        * softmax_scale
    )
    suffix_live = (jnp.arange(slot_count, dtype=jnp.int32)[None, :] < suffix_lens[:, None])[
        :, None, None, :
    ]
    suffix_scores = jnp.where(suffix_live, suffix_scores, floor_score)
    incoming_keys = new_keys.reshape(local_rows, KV, HD)
    incoming_values = new_values.reshape(local_rows, KV, HD)
    incoming_scores = (
        jnp.einsum(
            "iqnc,iqc->iqn", resident_heads, incoming_keys, preferred_element_type=jnp.float32
        )
        * softmax_scale
    )
    home_peak = jnp.maximum(jnp.max(suffix_scores, axis=3), incoming_scores)
    suffix_weights = jnp.where(suffix_live, jnp.exp(suffix_scores - home_peak[..., None]), 0.0)
    fresh_weights = jnp.exp(incoming_scores - home_peak)
    home_mass = jnp.sum(suffix_weights, axis=3) + fresh_weights
    resident_numerator = jnp.einsum(
        "bkgt,btkd->bkgd",
        suffix_weights.astype(jnp.bfloat16),
        own_values,
        preferred_element_type=jnp.float32,
    )
    resident_numerator = resident_numerator + jnp.einsum(
        "cqx,cqh->cqxh",
        fresh_weights.astype(jnp.bfloat16),
        incoming_values,
        preferred_element_type=jnp.float32,
    )
    home_out = (
        resident_numerator.reshape(local_rows, H, HD) / home_mass.reshape(local_rows, H)[..., None]
    )
    home_lse = (home_peak + jnp.log(home_mass)).reshape(local_rows, H)
    recv_out = lax.all_to_all(out_all, SEQ, split_axis=0, concat_axis=0, tiled=True)
    recv_lse = two_step_exchange(lse_all, ("seq_0", "seq_1"), (0, 1), 0, 0)
    recv_out = recv_out.reshape(owner_count, local_rows, H, HD).astype(jnp.float32)
    recv_lse = recv_lse.reshape(owner_count, local_rows, H)
    overall = jnp.maximum(jnp.max(recv_lse, axis=0), home_lse)
    factor = jnp.exp(recv_lse - overall[None])
    home_factor = jnp.exp(home_lse - overall)
    merged = jnp.sum(factor[..., None] * recv_out, axis=0) + home_factor[..., None] * home_out
    divisor = jnp.sum(factor, axis=0) + home_factor
    result = merged / divisor[..., None]
    return result.reshape(local_rows, H * HD).astype(jnp.bfloat16)


def solution(mesh):
    finer = Mesh(mesh.devices.reshape(mesh.shape["grp"], 16, 2), ("grp", "seq_0", "seq_1"))
    placed = (
        P(GRP_SEQ, None),
        P(GRP_SEQ, None),
        P(GRP_SEQ, None),
        P(GRP_SEQ, None, None),
        P(GRP_SEQ, None, None),
        P(GRP_SEQ),
        P(GRP_SEQ, None, None),
        P(GRP_SEQ, None, None),
        P("grp", None),
        P("grp"),
    )
    return jax.shard_map(
        local, mesh=finer, in_specs=placed, out_specs=P(GRP_SEQ, None), check_vma=False
    )
```

profile of v0, /device:TPU:70, one launch (start us, length us, event | category | flops | bytes accessed | tf_op | source)
XLA Modules:
  0.0 411.6 jit_solution(18046694975865880735)
XLA Ops:
  6.6 0.7 all-gather.2.cloned.1.call-update
  7.3 0.9 compare_reduce_fusion
  8.4 2.2 copy.106
  10.6 3.6 copy.107
  14.2 0.4 broadcast_compare_fusion
  14.6 70.8 %all-gather.2.cloned.1.call-done = bf16[512,4096]{1,0:T(8,128)(2,1)} async-done(((bf16[16,4096]{1,0:T(8,128)(2,1)}), bf16[512,4096]{1,0:T(8,128)(2,1)}) %all-gather.2.cloned.1.call-update) | async-done | bytes 4194320 | tf_op jit(solution)/shard_map/all_gather | solution.py:71
  85.4 6.5 %copy.78 = bf16[512,4096]{0,1:T(8,128)(2,1)} copy(bf16[512,4096]{1,0:T(8,128)(2,1)} %all-gather.2.cloned.1.call-done) | data formatting | bytes 8388608 | tf_op jit(solution)/shard_map/all_gather | solution.py:71
  91.9 27.0 %fusion = (f32[512,8,4]{0,2,1:T(4,128)S(1)}, f32[8,1024,512,4]{2,1,3,0:T(8,128)}) fusion(pred[512,1024]{0,1:T(8,128)(4,1)S(1)} %broadcast_compare_fusion, bf16[512,8,4,128]{0,3,2,1:T(8,128)(2,1)} %bitcast.83, bf16[1024,8,128,1]{2,1,0,3:T(8,128)(2,1)S(1)} %bitcast.84), kind=kOutput, calls=%fused_computation.2 | convolution fusion | flops 4345282560 | bytes 73990144 | tf_op jit(solution)/shard_map/bkgd,tkd->bkgt/dot_general | solution.py:75
  118.9 21.8 %fusion.2 = f32[512,8,4]{0,2,1:T(4,128)S(1)} fusion(f32[8,1024,512,4]{2,1,3,0:T(8,128)} %get-tuple-element.13, f32[512,8,4]{0,2,1:T(4,128)S(1)} %get-tuple-element.12, pred[512,1024]{0,1:T(8,128)(4,1)S(1)} %broadcast_compare_fusion), kind=kLoop, calls=%fused_computation.4 | loop fusion | flops 83869696 | bytes 67764224 | tf_op jit(solution)/shard_map/reduce_sum | solution.py:84
  140.7 0.8 copy.81
  141.5 2.3 add.44
  143.8 8.4 %all-to-all-start = ((f32[16,2,512]{2,1,0:T(2,128)}), f32[16,2,512]{2,1,0:T(2,128)S(1)}, u32[]{:S(2)}, u32[]{:S(2)}) async-start(f32[16,2,512]{2,1,0:T(2,128)} %add.44), calls=%async_computation | async-start | bytes 131072 | tf_op jit(solution)/shard_map/all_to_all | solution.py:35
  152.2 29.9 %fusion.12 = bf16[512,8,4,128]{3,0,2,1:T(8,128)(2,1)} fusion(f32[512,8,4]{0,2,1:T(4,128)S(1)} %fusion.2, f32[8,1024,512,4]{2,1,3,0:T(8,128)} %get-tuple-element.13, f32[512,8,4]{0,2,1:T(4,128)S(1)} %get-tuple-element.12, pred[512,1024]{0,1:T(8,128)(4,1)S(1)} %broadcast_compare_fusion, bf16[1024,8,128,1]{2,1,0,3:T(8,128)(2,1)} %bitcast.87), kind=kOutput, calls=%fused_computation.14 | convolution fusion | flops 4383047680 | bytes 74055680 | tf_op jit(solution)/shard_map/bkgt,tkd->bkgd/dot_general | solution.py:85
  182.1 7.3 %copy.89 = bf16[512,8,4,128]{3,2,1,0:T(4,128)(2,1)} copy(bf16[512,8,4,128]{3,0,2,1:T(8,128)(2,1)} %fusion.12) | data formatting | bytes 8388608 | tf_op jit(solution)/shard_map/convert_element_type | solution.py:91
  189.5 7.8 %all_to_all.14 = bf16[32,16,4096]{2,1,0:T(8,128)(2,1)} reshape(bf16[512,8,4,128]{3,2,1,0:T(4,128)(2,1)} %copy.89) | data formatting | bytes 8388608 | tf_op jit(solution)/shard_map/all_to_all | solution.py:136
  197.3 3.8 all_to_all.19
  201.1 13.1 %all-to-all-start.2 = ((bf16[32,16,4096]{2,1,0:T(8,128)(2,1)}), bf16[32,16,4096]{2,1,0:T(8,128)(2,1)}, u32[]{:S(2)}, u32[]{:S(2)}) async-start(bf16[32,16,4096]{2,1,0:T(8,128)(2,1)} %all_to_all.14), calls=%async_computation.2 | async-start | bytes 8388608 | tf_op jit(solution)/shard_map/all_to_all | solution.py:136
  214.5 0.3 fusion.44
  214.8 5.7 %fusion.43 = (f32[16,8,4]{2,1,0:T(8,128)S(1)}, f32[16,8,4,256]{3,2,1,0:T(4,128)S(1)}) fusion(bf16[16,8,4,128]{3,2,1,0:T(4,128)(2,1)S(1)} %reshape.158, pred[16,256]{1,0:T(8,128)(4,1)S(1)} %iota_compare_fusion, bf16[16,256,1024]{2,1,0:T(8,128)(2,1)} %param.13), kind=kOutput, calls=%fused_computation.53 | convolution fusion | flops 33947136 | bytes 9050112 | tf_op jit(solution)/shard_map/bkgd,btkd->bkgt/dot_general | solution.py:101
  220.6 0.4 fusion.28
  221.1 0.1 copy.85
  221.3 0.1 copy.92
  221.5 4.7 %fusion.21 = f32[16,8,4,128]{3,2,1,0:T(4,128)S(1)} fusion(f32[16,8,4,256]{3,2,1,0:T(4,128)S(1)} %get-tuple-element.15, f32[16,8,4]{2,1,0:T(8,128)S(1)} %get-tuple-element.6, pred[16,256]{1,0:T(8,128)(4,1)S(1)} %iota_compare_fusion, f32[16,8,128]{2,1,0:T(8,128)S(1)} %bitcast.98, f32[16,8,4]{2,1,0:T(8,128)S(1)} %get-tuple-element.5, ...), kind=kOutput, calls=%fused_computation.20 | convolution fusion | flops 34078720 | bytes 9248768 | tf_op jit(solution)/shard_map/bkgt,btkd->bkgd/dot_general | solution.py:120
  226.6 0.1 reshape_reshape_reshape.4
  226.9 4.6 %mul.68 = f32[32,16,32,128]{3,2,1,0:T(8,128)} broadcast(f32[32,16,32]{2,1,0:T(8,128)S(1)} %subtract_exponential_fusion), dimensions={0,1,2} | broadcast | bytes 8454144 | tf_op jit(solution)/shard_map/mul | solution.py:143
  231.4 9.4 %mul.69 = f32[32,16,4096]{2,1,0:T(8,128)} reshape(f32[32,16,32,128]{3,2,1,0:T(8,128)} %mul.68) | data formatting | bytes 16777216 | tf_op jit(solution)/shard_map/mul | solution.py:143
  240.8 156.7 %all-to-all-done.2 = bf16[32,16,4096]{2,1,0:T(8,128)(2,1)} async-done(((bf16[32,16,4096]{2,1,0:T(8,128)(2,1)}), bf16[32,16,4096]{2,1,0:T(8,128)(2,1)}, u32[]{:S(2)}, u32[]{:S(2)}) %all-to-all-start.2) | async-done | bytes 4194336 | tf_op jit(solution)/shard_map/all_to_all | solution.py:136
  397.6 5.7 %multiply_reduce_fusion = f32[16,4096]{1,0:T(8,128)S(1)} fusion(f32[32,16,4096]{2,1,0:T(8,128)} %mul.69, bf16[32,16,4096]{2,1,0:T(8,128)(2,1)} %all-to-all-done.2), kind=kLoop, calls=%fused_computation.15 | loop fusion | flops 6225920 | bytes 12845056 | tf_op jit(solution)/shard_map/reduce_sum | solution.py:143
  403.3 0.1 div.35
  403.4 0.1 div.38
  403.5 0.1 mul.71
  403.7 1.1 fusion.30
  (37 shorter events, 1.2 us)
Async XLA Ops:
  6.5 7.7 %copy-start.3 = (s32[512]{0:T(512)S(1)}, s32[512]{0:T(512)}, u32[]{:S(2)}) copy-start(s32[512]{0:T(512)} %param.19) | copy-start | bytes 6148
  6.5 78.8 %all-gather.2.cloned.1.call-start = ((), (), s32[]{:S(2)}) async-start(), calls=%async_computation.3 | async-start | bytes 4325376 | tf_op jit(solution)/shard_map/all_gather | solution.py:71
  143.8 53.5 %all-to-all-start = ((f32[16,2,512]{2,1,0:T(2,128)}), f32[16,2,512]{2,1,0:T(2,128)S(1)}, u32[]{:S(2)}, u32[]{:S(2)}) async-start(f32[16,2,512]{2,1,0:T(2,128)} %add.44), calls=%async_computation | async-start | bytes 131072 | tf_op jit(solution)/shard_map/all_to_all | solution.py:35
  189.5 24.8 %copy-start = (bf16[16,4096]{1,0:T(8,128)(2,1)S(1)}, bf16[16,4096]{1,0:T(8,128)(2,1)}, u32[]{:S(2)}) copy-start(bf16[16,4096]{1,0:T(8,128)(2,1)} %param.10) | copy-start | bytes 393220
  189.5 24.9 %copy-start.1 = (bf16[16,1024]{1,0:T(8,128)(2,1)S(1)}, bf16[16,1024]{1,0:T(8,128)(2,1)}, u32[]{:S(2)}) copy-start(bf16[16,1024]{1,0:T(8,128)(2,1)} %param.11) | copy-start | bytes 98308
  189.5 25.0 %copy-start.4 = (s32[16]{0:T(128)S(1)}, s32[16]{0:T(128)}, u32[]{:S(2)}) copy-start(s32[16]{0:T(128)} %param.15) | copy-start | bytes 196
  201.1 20.1 %copy-start.2 = (bf16[16,1024]{1,0:T(8,128)(2,1)S(1)}, bf16[16,1024]{1,0:T(8,128)(2,1)}, u32[]{:S(2)}) copy-start(bf16[16,1024]{1,0:T(8,128)(2,1)} %param.12) | copy-start | bytes 98308
  201.1 196.4 %all-to-all-start.2 = ((bf16[32,16,4096]{2,1,0:T(8,128)(2,1)}), bf16[32,16,4096]{2,1,0:T(8,128)(2,1)}, u32[]{:S(2)}, u32[]{:S(2)}) async-start(bf16[32,16,4096]{2,1,0:T(8,128)(2,1)} %all_to_all.14), calls=%async_computation.2 | async-start | bytes 8388608 | tf_op jit(solution)/shard_map/all_to_all | solution.py:136
Sparse Core Ops, SparseCore 0:
  9.1 76.2 all-gather.1
where the time goes:
time: 418 us; the launch traced here: 412 us
  waiting for transfers between devices  228 us (55%)
  matrix products  67.5 us (16%)
  local copies, waits for them, and re-layouts  46.3 us (11%)
  other arithmetic  30.6 us (7%)
  starting transfers between devices  21.5 us (5%)
  between operations  13.7 us (3%)
    all_to_all x1, waiting for transfers between devices, local(): lax.all_to_all(out_all, SEQ, split_axis=0, concat_axis=0, tiled=True)  157 us
    all_gather x1, waiting for transfers between devices, local(): shard_rows = lax.all_gather(queries, SEQ, axis=0, tiled=True)  70.8 us
    dot_general x1, matrix products, local(): jnp.einsum('bkgt,tkd->bkgd', weights.astype(jnp.bfloat16), values_local,...  29.9 us
    dot_general x1, matrix products, local(): jnp.einsum('bkgd,tkd->bkgt', query_head_count, keys_local, preferred_elem...  27 us
    reduce_sum x1, other arithmetic, local(): weight_sum = jnp.sum(weights, axis=3)  21.8 us
    mul x2, local copies, waits for them, and re-layouts, local(): factor[..., None] * recv_out  14 us
    all_to_all x1, starting transfers between devices, local(): lax.all_to_all(out_all, SEQ, split_axis=0, concat_axis=0, tiled=True)  13.1 us
    all_to_all x1, starting transfers between devices, moved_by_axis(): lax.all_to_all(tiles, axes[k], split_axis=k, concat_axis=k, tiled=True)  8.38 us
  transfers between devices with their start and end apart: 3, of which 2 were waited for; matrix products, arithmetic and copies ran while one was open for 17% of the time, Pallas kernels for 0%

commit v1 on v0

v1 whole, which is shorter than its diff:
```python
import functools
import math

import jax
import jax.numpy as jnp
from jax import lax
from jax.experimental import pallas as pl
from jax.experimental.pallas import tpu as pltpu
from jax.sharding import PartitionSpec as P

KV = 8
HD = 128
NPREF = 2
CORES = 2
PARTS = 4
LOW = -1e30
MESH = pl.DeviceIdType.MESH
F32 = jnp.float32
BF16 = jnp.bfloat16


def kernel(
    chips,
    c2,
    q_hbm,
    nk_ref,
    nv_ref,
    ks_hbm,
    vs_hbm,
    lens_ref,
    pk_hbm,
    pv_hbm,
    pen_ref,
    oh_ref,
    out_ref,
    qr,
    qp,
    kraw,
    vraw,
    kt,
    va,
    ko,
    vo,
    own,
    psend,
    precv,
    lown,
    lpsend,
    lprecv,
    rs,
    rss,
    rsd,
    rsds,
    qh,
    ho,
    hl,
    nk32,
    nv32,
    loc_sem,
    suf_sem,
    ring_send,
    ring_recv,
    qp_send,
    qp_recv,
    p_send,
    p_recv,
    ps_send,
    ps_recv,
    rs_send,
    rs_recv,
    rss_send,
    rss_recv,
):
    far = chips // 2
    rows = q_hbm.shape[0]
    width = q_hbm.shape[1] // PARTS
    heads = q_hbm.shape[1] // HD
    part_heads = heads // PARTS
    group = heads // KV
    part_kv = KV // PARTS
    half = rows // 2
    slots = ks_hbm.shape[1]

    me = lax.axis_index("seq")
    z, core = me // CORES, me % CORES
    right = {"seq": ((z + 1) % chips) * CORES + core}
    left = {"seq": ((z + chips - 1) % chips) * CORES + core}
    mate = {"seq": z * CORES + (1 - core)}

    def remote(src, dst, send, recv, device):
        return pltpu.make_async_remote_copy(
            src_ref=src, dst_ref=dst, send_sem=send, recv_sem=recv, device_id=device, device_id_type=MESH
        )

    q_in = [
        pltpu.make_async_copy(q_hbm.at[:, pl.ds(s * width, width)], qr.at[far - 1, s, 1], loc_sem.at[s])
        for s in range(PARTS)
    ]
    k_in = pltpu.make_async_copy(pk_hbm, kraw, loc_sem.at[PARTS])
    v_in = pltpu.make_async_copy(pv_hbm, vraw, loc_sem.at[PARTS + 1])
    for copy in q_in:
        copy.start()
    k_in.start()
    v_in.start()

    def suffix_copies(b):
        return (
            pltpu.make_async_copy(ks_hbm.at[b], ko.at[b], suf_sem.at[0, b]),
            pltpu.make_async_copy(vs_hbm.at[b], vo.at[b], suf_sem.at[1, b]),
        )

    barrier = pltpu.get_barrier_semaphore()
    for device in (left, right, mate):
        pl.semaphore_signal(barrier, inc=1, device_id=device, device_id_type=MESH)
    pl.semaphore_wait(barrier, 3)

    def ring_copy(direction, source, slot, s):
        return remote(
            source,
            qr.at[slot, s, direction],
            ring_send.at[direction, s],
            ring_recv.at[direction, slot, s],
            right if direction == 0 else left,
        )

    def mate_queries(slot, s):
        return remote(qr.at[slot, s], qp.at[slot, s], qp_send.at[s], qp_recv.at[slot, s], mate)

    def mate_partial(slot, s):
        return remote(psend.at[slot, s], precv.at[slot, s], p_send.at[s], p_recv.at[slot, s], mate)

    def mate_stats(slot):
        return remote(lpsend.at[slot], lprecv.at[slot], ps_send, ps_recv.at[slot], mate)

    for s in range(PARTS):
        q_in[s].wait()
        for direction in (0, 1):
            ring_copy(direction, qr.at[far - 1, s, 1], 0, s).start()

    @pl.loop(0, rows)
    def _(b):
        for copy in suffix_copies(b):
            copy.start()

    lown[...] = jnp.zeros_like(lown)
    lpsend[...] = jnp.zeros_like(lpsend)
    for direction, k in ((0, far + 1), (1, far), (1, far + 1)):
        rs[direction, k] = jnp.zeros(rs.shape[2:], rs.dtype)
        rss[direction, k] = jnp.full(rss.shape[2:], LOW, F32)

    k_in.wait()

    @pl.loop(0, KV)
    def _(h):
        columns = pl.ds(pl.multiple_of(h * HD, HD), HD)
        kt[h, 0:HD, :] = kraw[:, columns].T
        kt[h, HD:, :] = pen_ref[...]

    v_in.wait()

    @pl.loop(0, KV)
    def _(h):
        columns = pl.ds(pl.multiple_of(h * HD, HD), HD)
        va[h, :, 0:HD] = vraw[:, columns]
        va[h, :, HD:] = jnp.ones((va.shape[1], HD), BF16)

    for s in range(PARTS):
        for i in range(part_heads):
            qh[pl.ds(s * part_heads + i, rows, stride=heads), :] = qr[far - 1, s, 1, :, i * HD : (i + 1) * HD].astype(F32)
    nk32[...] = nk_ref[...].astype(F32)
    nv32[...] = nv_ref[...].astype(F32)

    lane = lax.broadcasted_iota(jnp.int32, (half, HD), 1)

    def attend(slot, s):
        k = slot + 1
        chip_of = ((z + chips - k) % chips, jnp.where(k == far, z, (z + k) % chips))
        onehots = [oh_ref[chip_of[d] * CORES + (core if src == 0 else 1 - core)] for src in (0, 1) for d in (0, 1)]
        stats = [lown[slot, 0], lown[slot, 1], lpsend[slot, 0], lpsend[slot, 1]]
        for i in range(part_kv):
            h = s * part_kv + i
            tiles = []
            for src, ref in enumerate((qr, qp)):
                for d in (0, 1):
                    for g in range(group):
                        at = (i * group + g) * HD
                        tiles.append(jnp.concatenate([ref[slot, s, d, :, at : at + HD], onehots[src * 2 + d]], axis=1))
            qa = jnp.concatenate(tiles, axis=0)
            score = jnp.dot(qa, kt[h], preferred_element_type=F32)
            peak = jnp.max(score, axis=1, keepdims=True)
            weight = jnp.exp2((score - peak) * c2).astype(BF16)
            summed = jnp.dot(weight, va[h], preferred_element_type=F32)
            mass = summed[:, HD:]
            part = summed[:, :HD] / mass
            lse = peak * c2 + jnp.log2(mass)
            for src in (0, 1):
                for d in (0, 1):
                    for g in range(group):
                        row = ((src * 2 + d) * group + g) * rows
                        at = (i * group + g) * HD
                        tile = part[row : row + rows]
                        if src == 0:
                            own[slot, s, d, :, at : at + HD] = tile
                        else:
                            psend[slot, s, d, :, at : at + HD] = tile.astype(BF16)
                        head = s * part_heads + i * group + g
                        n = src * 2 + d
                        stats[n] = jnp.where(lane == head, lse[row : row + half], stats[n])
                        stats[n] = jnp.where(lane == head + heads, lse[row + half : row + rows], stats[n])
        lown[slot, 0], lown[slot, 1], lpsend[slot, 0], lpsend[slot, 1] = stats

    def attend_and_send(slot, s):
        mate_queries(slot, s).wait_recv()
        attend(slot, s)

        @pl.when(slot >= 1)
        def _():
            mate_partial(slot, s).wait_send()

        mate_partial(slot, s).start()

        @pl.when(s == PARTS - 1)
        def _():
            @pl.when(slot >= 1)
            def _():
                mate_stats(slot).wait_send()

            mate_stats(slot).start()

    @pl.loop(0, far * PARTS)
    def _(step):
        slot, s = step // PARTS, step % PARTS
        ring_copy(0, qr.at[slot, s, 0], slot, s).wait_recv()

        @pl.when(slot < far - 1)
        def _():
            onward = ring_copy(0, qr.at[slot, s, 0], slot + 1, s)
            onward.wait_send()
            onward.start()
            ring_copy(1, qr.at[slot, s, 1], slot, s).wait_recv()

        @pl.when(slot < far - 2)
        def _():
            onward = ring_copy(1, qr.at[slot, s, 1], slot + 1, s)
            onward.wait_send()
            onward.start()

        @pl.when(slot >= 1)
        def _():
            mate_queries(slot, s).wait_send()

        mate_queries(slot, s).start()

        @pl.when(step >= 1)
        def _():
            attend_and_send((step - 1) // PARTS, (step - 1) % PARTS)

    attend_and_send(far - 1, PARTS - 1)

    for s in range(PARTS):
        ring_copy(0, qr.at[0, s, 0], 0, s).wait_send()
        ring_copy(1, qr.at[0, s, 1], 0, s).wait_send()
        mate_queries(0, s).wait_send()
        mate_partial(0, s).wait_send()
    mate_stats(0).wait_send()

    def stat_copy(direction, k):
        return remote(
            rsds.at[direction, k],
            rss.at[direction, k],
            rss_send.at[direction],
            rss_recv.at[direction, k],
            left if direction == 0 else right,
        )

    def part_copy(direction, k, s):
        return remote(
            rsd.at[direction, k, s],
            rs.at[direction, k, s],
            rs_send.at[direction, s],
            rs_recv.at[direction, k, s],
            left if direction == 0 else right,
        )

    def across(tile, i):
        low = jnp.broadcast_to(tile[:, i : i + 1], (half, HD))
        high = jnp.broadcast_to(tile[:, heads + i : heads + i + 1], (half, HD))
        return jnp.concatenate([low, high], axis=0)

    def shares(stats):
        top = functools.reduce(jnp.maximum, stats)
        total = top + jnp.log2(sum(jnp.exp2(s - top) for s in stats))
        return total, [jnp.exp2(s - total) for s in stats[1:]]

    row_of = lax.broadcasted_iota(jnp.int32, (heads, KV * HD), 0)
    col_of = lax.broadcasted_iota(jnp.int32, (heads, KV * HD), 1)
    sub = lax.broadcasted_iota(jnp.int32, (2 * group, HD), 0)

    def home(b):
        for copy in suffix_copies(b):
            copy.wait()
        at = pl.ds(pl.multiple_of(b * heads, heads), heads)
        wide = jnp.concatenate([qh[at, :]] * KV, axis=1)
        wide = jnp.where(row_of // group == col_of // HD, wide, 0.0)
        score = lax.dot_general(
            wide.astype(BF16), ko[b], (((1,), (1,)), ((), ())), preferred_element_type=F32
        )
        slot_of = lax.broadcasted_iota(jnp.int32, (heads, slots), 1)
        score = jnp.where(slot_of < lens_ref[b], score, LOW)
        fresh = jnp.sum(wide * nk32[pl.ds(b, 1), :], axis=1, keepdims=True)
        peak = jnp.maximum(jnp.max(score, axis=1, keepdims=True), fresh)
        weight = jnp.exp2((score - peak) * c2)
        fresh = jnp.exp2((fresh - peak) * c2)
        mass = jnp.sum(weight, axis=1, keepdims=True) + fresh
        summed = jnp.dot(weight.astype(BF16), vo[b], preferred_element_type=F32)
        summed = summed + fresh.astype(BF16).astype(F32) * nv32[pl.ds(b, 1), :]
        picked = []
        for i in range(KV // 2):
            r = slice(2 * i * group, 2 * (i + 1) * group)
            first = summed[r, 2 * i * HD : (2 * i + 1) * HD]
            second = summed[r, (2 * i + 1) * HD : (2 * i + 2) * HD]
            picked.append(jnp.where(sub < group, first, second))
        ho[at, :] = jnp.concatenate(picked, axis=0) / mass
        hl[at, :] = jnp.broadcast_to(peak * c2 + jnp.log2(mass), (heads, HD))

    per_step = -(-rows // far)

    @pl.loop(0, far)
    def _(j):
        k = far - j
        slot = k - 1
        mate_stats(slot).wait_recv()

        @pl.when(k < far)
        def _():
            stat_copy(0, k + 1).wait_recv()

        @pl.when(k < far - 1)
        def _():
            stat_copy(1, k + 1).wait_recv()

        factors = []
        for d in (0, 1):
            total, weights = shares([lown[slot, d], lprecv[slot, d], rss[d, k + 1]])
            rsds[d, k] = total
            factors.append(weights)

        @pl.when(k < far)
        def _():
            stat_copy(0, k).wait_send()

        stat_copy(0, k).start()

        @pl.when(k < far - 1)
        def _():
            stat_copy(1, k).wait_send()

        @pl.when(k < far)
        def _():
            stat_copy(1, k).start()

        for s in range(PARTS):
            mate_partial(slot, s).wait_recv()

            @pl.when(k < far)
            def _():
                part_copy(0, k + 1, s).wait_recv()

            @pl.when(k < far - 1)
            def _():
                part_copy(1, k + 1, s).wait_recv()

            for d in (0, 1):
                for i in range(part_heads):
                    at = slice(i * HD, (i + 1) * HD)
                    head = s * part_heads + i
                    mine = own[slot, s, d, :, at]
                    merged = mine + across(factors[d][0], head) * (precv[slot, s, d, :, at].astype(F32) - mine)
                    merged = merged + across(factors[d][1], head) * (rs[d, k + 1, s, :, at].astype(F32) - mine)
                    rsd[d, k, s, :, at] = merged.astype(BF16)

                if d == 0:

                    @pl.when(k < far)
                    def _():
                        part_copy(0, k, s).wait_send()

                    part_copy(0, k, s).start()
                else:

                    @pl.when(k < far - 1)
                    def _():
                        part_copy(1, k, s).wait_send()

                    @pl.when(k < far)
                    def _():
                        part_copy(1, k, s).start()

        for n in range(per_step):
            b = j * per_step + n

            @pl.when(b < rows)
            def _():
                home(b)

    for d in (0, 1):
        stat_copy(d, 1).wait_recv()
    total, weights = shares([lown[far - 1, 1], lprecv[far - 1, 1], rss[0, 1], rss[1, 1]])
    for s in range(PARTS):
        for d in (0, 1):
            part_copy(d, 1, s).wait_recv()
        for i in range(part_heads):
            at = slice(i * HD, (i + 1) * HD)
            head = s * part_heads + i
            mine = own[far - 1, s, 1, :, at]
            merged = mine + across(weights[0], head) * (precv[far - 1, s, 1, :, at].astype(F32) - mine)
            merged = merged + across(weights[1], head) * (rs[0, 1, s, :, at].astype(F32) - mine)
            merged = merged + across(weights[2], head) * (rs[1, 1, s, :, at].astype(F32) - mine)
            home_lse = hl[pl.ds(head, rows, stride=heads), :]
            home_out = ho[pl.ds(head, rows, stride=heads), :]
            share = 1.0 / (1.0 + jnp.exp2(across(total, head) - home_lse))
            merged = merged + share * (home_out - merged)
            out_ref[:, s * width + i * HD : s * width + (i + 1) * HD] = merged.astype(BF16)

    for d in (0, 1):
        stat_copy(d, 1).wait_send()
        for s in range(PARTS):
            part_copy(d, 1, s).wait_send()


def local(
    queries,
    new_keys,
    new_values,
    suffix_keys,
    suffix_values,
    suffix_lens,
    prefix_keys,
    prefix_values,
    page_table,
    prefix_id,
):
    devices = lax.axis_size("seq")
    chips = devices // CORES
    far = chips // 2
    rows, columns = queries.shape
    width = columns // PARTS
    heads = columns // HD
    pages, page, kv_columns = prefix_keys.shape
    tokens = pages * page
    slots = suffix_keys.shape[1]
    half = rows // 2

    ids = lax.axis_index("seq") * pages + jnp.arange(pages, dtype=jnp.int32)
    held = jnp.any(page_table[:, :, None] == ids[None, None, :], axis=1)
    penalty = jnp.where(held, 0.0, LOW).astype(BF16)
    penalty = jnp.repeat(penalty, page, axis=1)
    penalty = jnp.concatenate([penalty, jnp.zeros((HD - NPREF, tokens), BF16)], axis=0)
    onehot = (prefix_id[:, None] == jnp.arange(HD, dtype=jnp.int32)[None, :]).astype(BF16)
    onehot = onehot.reshape(devices, rows, HD)

    any_space = pl.BlockSpec(memory_space=pl.ANY)
    vmem = pl.BlockSpec(memory_space=pltpu.VMEM)
    smem = pl.BlockSpec(memory_space=pltpu.SMEM)
    dma = pltpu.SemaphoreType.DMA
    chunk = (PARTS, 2, rows, width)
    return pl.pallas_call(
        functools.partial(kernel, chips, math.log2(math.e) / math.sqrt(HD)),
        out_shape=jax.ShapeDtypeStruct((rows, columns), BF16),
        in_specs=[any_space, vmem, vmem, any_space, any_space, smem, any_space, any_space, vmem, vmem],
        out_specs=vmem,
        scratch_shapes=[
            pltpu.VMEM((far, *chunk), BF16),
            pltpu.VMEM((far, *chunk), BF16),
            pltpu.VMEM((tokens, kv_columns), BF16),
            pltpu.VMEM((tokens, kv_columns), BF16),
            pltpu.VMEM((KV, 2 * HD, tokens), BF16),
            pltpu.VMEM((KV, tokens, 2 * HD), BF16),
            pltpu.VMEM((rows, slots, kv_columns), BF16),
            pltpu.VMEM((rows, slots, kv_columns), BF16),
            pltpu.VMEM((far, *chunk), F32),
            pltpu.VMEM((far, *chunk), BF16),
            pltpu.VMEM((far, *chunk), BF16),
            pltpu.VMEM((far, 2, half, HD), F32),
            pltpu.VMEM((far, 2, half, HD), F32),
            pltpu.VMEM((far, 2, half, HD), F32),
            pltpu.VMEM((2, far + 2, PARTS, rows, width), BF16),
            pltpu.VMEM((2, far + 2, half, HD), F32),
            pltpu.VMEM((2, far + 1, PARTS, rows, width), BF16),
            pltpu.VMEM((2, far + 1, half, HD), F32),
            pltpu.VMEM((rows * heads, HD), F32),
            pltpu.VMEM((rows * heads, HD), F32),
            pltpu.VMEM((rows * heads, HD), F32),
            pltpu.VMEM((rows, kv_columns), F32),
            pltpu.VMEM((rows, kv_columns), F32),
            dma((PARTS + 2,)),
            dma((2, rows)),
            dma((2, PARTS)),
            dma((2, far, PARTS)),
            dma((PARTS,)),
            dma((far, PARTS)),
            dma((PARTS,)),
            dma((far, PARTS)),
            dma,
            dma((far,)),
            dma((2, PARTS)),
            dma((2, far + 2, PARTS)),
            dma((2,)),
            dma((2, far + 2)),
        ],
        compiler_params=pltpu.CompilerParams(
            collective_id=0, has_side_effects=True, vmem_limit_bytes=64000000
        ),
    )(
        queries,
        new_keys,
        new_values,
        suffix_keys,
        suffix_values,
        suffix_lens,
        prefix_keys.reshape(tokens, kv_columns),
        prefix_values.reshape(tokens, kv_columns),
        penalty,
        onehot,
    )


def solution(mesh):
    spread = ("grp", "seq")
    placed = (
        P(spread, None),
        P(spread, None),
        P(spread, None),
        P(spread, None, None),
        P(spread, None, None),
        P(spread),
        P(spread, None, None),
        P(spread, None, None),
        P("grp", None),
        P("grp"),
    )
    return jax.shard_map(local, mesh=mesh, in_specs=placed, out_specs=P(spread, None), check_vma=False)
```

time: 418 us -> 100 us (0.24); the launches traced: 412 us -> 99.9 us
  waiting for transfers between devices: 228 us -> 0 us
  Pallas kernels: 0 us -> 94.9 us
  matrix products: 67.5 us -> 0 us
  local copies, waits for them, and re-layouts: 46.3 us -> 3.23 us
  other arithmetic: 30.6 us -> 1.72 us
  starting transfers between devices: 21.5 us -> 0 us
  between operations: 13.7 us -> 0.03 us
    all_to_all x2 -> x0, waiting for transfers between devices: 157 us -> none  [the longest x1 157 us: local(): lax.all_to_all(out_all, SEQ, split_axis=0, concat_axis=0, tiled=True)]
    pallas_call x0 -> x1, Pallas kernels: none -> 94.9 us  [local(): pl.pallas_call(functools.partial(kernel, chips, math.log2(math.e) / math....]
    all_gather x1 -> x0, waiting for transfers between devices: 70.8 us -> none  [local(): shard_rows = lax.all_gather(queries, SEQ, axis=0, tiled=True)]
    dot_general x5 -> x0, matrix products: 67.5 us -> none  [the longest x1 29.9 us: local(): jnp.einsum('bkgt,tkd->bkgd', weights.astype(jnp.bfloat16), values_local,...]
    reduce_sum x5 -> x0, other arithmetic: 27.9 us -> none  [the longest x1 21.8 us: local(): weight_sum = jnp.sum(weights, axis=3)]
    all_to_all x2 -> x0, starting transfers between devices: 21.5 us -> none  [the longest x1 13.1 us: local(): lax.all_to_all(out_all, SEQ, split_axis=0, concat_axis=0, tiled=True)]
    mul x3 -> x0, local copies, waits for them, and re-layouts: 14.1 us -> none  [the longest x2 14 us: local(): factor[..., None] * recv_out]
    all_to_all x3 -> x0, local copies, waits for them, and re-layouts: 7.9 us -> none  [the longest x1 7.83 us: local(): lax.all_to_all(out_all, SEQ, split_axis=0, concat_axis=0, tiled=True)]
  transfers between devices with their start and end apart: 3 -> 0, of which waited for: 2 -> 0; matrix products, arithmetic and copies ran while one was open for 17% -> 0% of each run, Pallas kernels for 0% -> 0%
where the time goes in v1:
time: 100 us; the launch traced here: 99.9 us
  Pallas kernels  94.9 us (95%)
  local copies, waits for them, and re-layouts  3.23 us (3%)
  other arithmetic  1.72 us (2%)
    pallas_call x1, Pallas kernels, local(): pl.pallas_call(functools.partial(kernel, chips, math.log2(math.e) / math....  94.9 us

profile of v1, /device:TPU:70, one launch (start us, length us, event | category | flops | bytes accessed | tf_op | source)
XLA Modules:
  0.0 99.9 jit_solution(12830127910224754467)
XLA Ops:
  0.0 0.9 compare_reduce_fusion
  0.9 0.8 eq.32
  1.7 0.1 broadcast_in_dim.18
  1.8 0.1 reshape.26
  1.9 0.8 fusion.oh_ref
  2.7 0.7 concatenate.3.pen_ref
  3.4 94.9 %shard_map.100 = bf16[16,4096]{1,0:T(8,128)(2,1)} custom-call(bf16[16,4096]{1,0:T(8,128)(2,1)} %q_hbm.1, bf16[16,1024]{1,0:T(8,128)(2,1)} %nk_ref.1, bf16[16,1024]{1,0:T(8,128)(2,1)} %nv_ref.1, bf16[16,256,1024]{2,1,0:T(8,128)(2,1)} %ks_hbm.1, bf16[16,256,1024]{2,1,0:T(8,128)(2,1)} %vs_hbm.1, s32[16]{0:T(128)} %lens_ref.1, bf16[1024,1024]{1,0:T(8,128)(2,1)} %bitcast.2, ...), custom_call_target="tpu_custom_call" | custom-call | tf_op jit(solution)/shard_map/pallas_call | solution.py:467
  98.3 1.6 %copy.12 = bf16[16,4096]{1,0:T(8,128)(2,1)} copy(bf16[16,4096]{1,0:T(8,128)(2,1)} %shard_map.100) | data formatting | bytes 262144
  (2 shorter events, 0.0 us)

commit v2 on v1

--- a/solution.py
+++ b/solution.py
@@ -13,6 +13,7 @@
 NPREF = 2
 CORES = 2
 PARTS = 4
+HALF = PARTS // 2
 LOW = -1e30
 MESH = pl.DeviceIdType.MESH
 F32 = jnp.float32
@@ -22,6 +23,7 @@
 def kernel(
     chips,
     c2,
+    page_size,
     q_hbm,
     nk_ref,
     nv_ref,
@@ -30,14 +32,18 @@
     lens_ref,
     pk_hbm,
     pv_hbm,
-    pen_ref,
-    oh_ref,
+    table_ref,
+    pid_ref,
     out_ref,
     qr,
     qp,
     kraw,
     vraw,
     kt,
+    oh,
+    even,
+    odd,
+    weight_of,
     va,
     ko,
     vo,
@@ -80,11 +86,12 @@
     part_kv = KV // PARTS
     half = rows // 2
     slots = ks_hbm.shape[1]
+    pages = kraw.shape[0] // page_size
 
     me = lax.axis_index("seq")
     z, core = me // CORES, me % CORES
-    right = {"seq": ((z + 1) % chips) * CORES + core}
-    left = {"seq": ((z + chips - 1) % chips) * CORES + core}
+    right = {"seq": ((z + 1) % chips) * CORES + 1 - core}
+    left = {"seq": ((z + chips - 1) % chips) * CORES + 1 - core}
     mate = {"seq": z * CORES + (1 - core)}
 
     def remote(src, dst, send, recv, device):
@@ -137,16 +144,34 @@
         for direction in (0, 1):
             ring_copy(direction, qr.at[far - 1, s, 1], 0, s).start()
 
-    @pl.loop(0, rows)
-    def _(b):
-        for copy in suffix_copies(b):
-            copy.start()
-
     lown[...] = jnp.zeros_like(lown)
     lpsend[...] = jnp.zeros_like(lpsend)
-    for direction, k in ((0, far + 1), (1, far), (1, far + 1)):
-        rs[direction, k] = jnp.zeros(rs.shape[2:], rs.dtype)
-        rss[direction, k] = jnp.full(rss.shape[2:], LOW, F32)
+    for d in (0, 1):
+        rs[d, far + 1] = jnp.zeros(rs.shape[2:], rs.dtype)
+        rss[d, far + 1] = jnp.full(rss.shape[2:], LOW, F32)
+        for s in range(PARTS):
+            if s // HALF != d:
+                rs[d, far, s] = jnp.zeros(rs.shape[3:], rs.dtype)
+
+    tokens = kraw.shape[0]
+    mine_of = me * pages + lax.broadcasted_iota(jnp.int32, (pages, table_ref.shape[1]), 0)
+    column = lax.broadcasted_iota(jnp.int32, (pages, HD), 1)
+    missing = jnp.zeros((pages, HD), F32)
+    for p in range(NPREF):
+        hit = jnp.where(table_ref[p : p + 1, :] == mine_of, 1.0, 0.0)
+        hit = jnp.max(hit, axis=1, keepdims=True)
+        missing = jnp.where(column == p, 1.0 - hit, missing)
+    page_of = lax.broadcasted_iota(jnp.int32, (pages, tokens), 1) // page_size
+    spread = jnp.where(page_of == lax.broadcasted_iota(jnp.int32, (pages, tokens), 0), 1.0, 0.0).astype(BF16)
+    penalty = jnp.dot(missing.T.astype(BF16), spread, preferred_element_type=F32)
+    penalty = jnp.where(penalty > 0.5, LOW, 0.0).astype(BF16)
+
+    ids = pid_ref[...].astype(F32)
+    ids = jnp.concatenate([ids, jnp.zeros((HD - ids.shape[0], HD), F32)], axis=0).T
+    choice = lax.broadcasted_iota(jnp.int32, (HD, HD), 1).astype(F32)
+    for n in range(pid_ref.shape[0]):
+        flags = jnp.where(choice == jnp.broadcast_to(ids[:, n : n + 1], (HD, HD)), 1.0, 0.0)
+        oh[n * HD : (n + 1) * HD, :] = flags.astype(BF16)
 
     k_in.wait()
 
@@ -154,7 +179,7 @@
     def _(h):
         columns = pl.ds(pl.multiple_of(h * HD, HD), HD)
         kt[h, 0:HD, :] = kraw[:, columns].T
-        kt[h, HD:, :] = pen_ref[...]
+        kt[h, HD:, :] = penalty
 
     v_in.wait()
 
@@ -164,6 +189,11 @@
         va[h, :, 0:HD] = vraw[:, columns]
         va[h, :, HD:] = jnp.ones((va.shape[1], HD), BF16)
 
+    @pl.loop(0, rows)
+    def _(b):
+        for copy in suffix_copies(b):
+            copy.start()
+
     for s in range(PARTS):
         for i in range(part_heads):
             qh[pl.ds(s * part_heads + i, rows, stride=heads), :] = qr[far - 1, s, 1, :, i * HD : (i + 1) * HD].astype(F32)
@@ -172,27 +202,36 @@
 
     lane = lax.broadcasted_iota(jnp.int32, (half, HD), 1)
 
-    def attend(slot, s):
+    def score_into(step, score):
+        slot, s = step // PARTS, step % PARTS
         k = slot + 1
         chip_of = ((z + chips - k) % chips, jnp.where(k == far, z, (z + k) % chips))
-        onehots = [oh_ref[chip_of[d] * CORES + (core if src == 0 else 1 - core)] for src in (0, 1) for d in (0, 1)]
-        stats = [lown[slot, 0], lown[slot, 1], lpsend[slot, 0], lpsend[slot, 1]]
+        came = [(core + k) % CORES, jnp.where(k == far, core, (core + k) % CORES)]
+        onehots = []
+        for src in (0, 1):
+            for d in (0, 1):
+                device = chip_of[d] * CORES + (came[d] if src == 0 else 1 - came[d])
+                onehots.append(oh[pl.ds(pl.multiple_of(device * rows, rows), rows), :])
         for i in range(part_kv):
-            h = s * part_kv + i
             tiles = []
             for src, ref in enumerate((qr, qp)):
                 for d in (0, 1):
                     for g in range(group):
                         at = (i * group + g) * HD
                         tiles.append(jnp.concatenate([ref[slot, s, d, :, at : at + HD], onehots[src * 2 + d]], axis=1))
-            qa = jnp.concatenate(tiles, axis=0)
-            score = jnp.dot(qa, kt[h], preferred_element_type=F32)
-            peak = jnp.max(score, axis=1, keepdims=True)
-            weight = jnp.exp2((score - peak) * c2).astype(BF16)
-            summed = jnp.dot(weight, va[h], preferred_element_type=F32)
-            mass = summed[:, HD:]
-            part = summed[:, :HD] / mass
-            lse = peak * c2 + jnp.log2(mass)
+            score[i] = jnp.dot(jnp.concatenate(tiles, axis=0), kt[s * part_kv + i], preferred_element_type=F32)
+
+    def weigh(step, score):
+        slot, s = step // PARTS, step % PARTS
+        stats = [lown[slot, 0], lown[slot, 1], lpsend[slot, 0], lpsend[slot, 1]]
+        peaks = [jnp.max(score[i], axis=1, keepdims=True) for i in range(part_kv)]
+        for i in range(part_kv):
+            weight_of[i] = jnp.exp2((score[i] - peaks[i]) * c2).astype(BF16)
+        sums = [jnp.dot(weight_of[i], va[s * part_kv + i], preferred_element_type=F32) for i in range(part_kv)]
+        for i in range(part_kv):
+            mass = sums[i][:, HD:]
+            part = sums[i][:, :HD] / mass
+            lse = peaks[i] * c2 + jnp.log2(mass)
             for src in (0, 1):
                 for d in (0, 1):
                     for g in range(group):
@@ -209,9 +248,8 @@
                         stats[n] = jnp.where(lane == head + heads, lse[row + half : row + rows], stats[n])
         lown[slot, 0], lown[slot, 1], lpsend[slot, 0], lpsend[slot, 1] = stats
 
-    def attend_and_send(slot, s):
-        mate_queries(slot, s).wait_recv()
-        attend(slot, s)
+    def send_partial(step):
+        slot, s = step // PARTS, step % PARTS
 
         @pl.when(slot >= 1)
         def _():
@@ -227,23 +265,39 @@
 
             mate_stats(slot).start()
 
-    @pl.loop(0, far * PARTS)
-    def _(step):
+    def far_copy(direction, source, s):
+        return remote(
+            source,
+            qr.at[far - 1, s, 0],
+            ring_send.at[direction, s],
+            ring_recv.at[direction, far - 1, s],
+            right if direction == 0 else left,
+        )
+
+    def forward(step):
         slot, s = step // PARTS, step % PARTS
-        ring_copy(0, qr.at[slot, s, 0], slot, s).wait_recv()
-
-        @pl.when(slot < far - 1)
-        def _():
-            onward = ring_copy(0, qr.at[slot, s, 0], slot + 1, s)
-            onward.wait_send()
-            onward.start()
-            ring_copy(1, qr.at[slot, s, 1], slot, s).wait_recv()
-
-        @pl.when(slot < far - 2)
-        def _():
-            onward = ring_copy(1, qr.at[slot, s, 1], slot + 1, s)
-            onward.wait_send()
-            onward.start()
+        for d in (0, 1):
+            carries = s // HALF == d
+
+            @pl.when(slot < far - 1)
+            def _():
+                ring_copy(d, qr.at[slot, s, d], slot, s).wait_recv()
+
+            @pl.when(slot < far - 2)
+            def _():
+                onward = ring_copy(d, qr.at[slot, s, d], slot + 1, s)
+                onward.wait_send()
+                onward.start()
+
+            @pl.when((slot == far - 2) & carries)
+            def _():
+                onward = far_copy(d, qr.at[slot, s, d], s)
+                onward.wait_send()
+                onward.start()
+
+            @pl.when((slot == far - 1) & carries)
+            def _():
+                far_copy(d, qr.at[0, s, d], s).wait_recv()
 
         @pl.when(slot >= 1)
         def _():
@@ -251,11 +305,30 @@
 
         mate_queries(slot, s).start()
 
-        @pl.when(step >= 1)
+    def advance(step, into, ready):
+        mate_queries((step - 1) // PARTS, (step - 1) % PARTS).wait_recv()
+        score_into(step - 1, into)
+        weigh(jnp.maximum(step - 2, 0), ready)
+
+        @pl.when(step >= 2)
         def _():
-            attend_and_send((step - 1) // PARTS, (step - 1) % PARTS)
-
-    attend_and_send(far - 1, PARTS - 1)
+            send_partial(step - 2)
+
+    @pl.loop(0, far * PARTS // 2)
+    def _(pair):
+        forward(2 * pair)
+
+        @pl.when(pair >= 1)
+        def _():
+            advance(2 * pair, odd, even)
+
+        forward(2 * pair + 1)
+        advance(2 * pair + 1, even, odd)
+
+    last = jnp.int32(far * PARTS)
+    advance(last, odd, even)
+    weigh(last - 1, odd)
+    send_partial(last - 1)
 
     for s in range(PARTS):
         ring_copy(0, qr.at[0, s, 0], 0, s).wait_send()
@@ -325,6 +398,8 @@
 
     per_step = -(-rows // far)
 
+    part_half = lane % heads // (HALF * part_heads)
+
     @pl.loop(0, far)
     def _(j):
         k = far - j
@@ -333,68 +408,53 @@
 
         @pl.when(k < far)
         def _():
-            stat_copy(0, k + 1).wait_recv()
-
-        @pl.when(k < far - 1)
-        def _():
-            stat_copy(1, k + 1).wait_recv()
+            for d in (0, 1):
+                stat_copy(d, k + 1).wait_recv()
 
         factors = []
+        side = [jnp.where(k == far, 0, d) for d in (0, 1)]
         for d in (0, 1):
-            total, weights = shares([lown[slot, d], lprecv[slot, d], rss[d, k + 1]])
-            rsds[d, k] = total
+            total, weights = shares([lown[slot, side[d]], lprecv[slot, side[d]], rss[d, k + 1]])
+            rsds[d, k] = jnp.where((part_half == d) | (k < far), total, LOW)
             factors.append(weights)
-
-        @pl.when(k < far)
-        def _():
-            stat_copy(0, k).wait_send()
-
-        stat_copy(0, k).start()
-
-        @pl.when(k < far - 1)
-        def _():
-            stat_copy(1, k).wait_send()
-
-        @pl.when(k < far)
-        def _():
-            stat_copy(1, k).start()
-
-        for s in range(PARTS):
-            mate_partial(slot, s).wait_recv()
+        for d in (0, 1):
 
             @pl.when(k < far)
             def _():
-                part_copy(0, k + 1, s).wait_recv()
-
-            @pl.when(k < far - 1)
-            def _():
-                part_copy(1, k + 1, s).wait_recv()
-
+                stat_copy(d, k).wait_send()
+
+            stat_copy(d, k).start()
+
+        for n in range(PARTS):
             for d in (0, 1):
+                s = (n + d * HALF) % PARTS
+                carries = s // HALF == d
+                if n < HALF:
+                    mate_partial(slot, s).wait_recv()
+
+                @pl.when(k < (far if carries else far - 1))
+                def _():
+                    part_copy(d, k + 1, s).wait_recv()
+
                 for i in range(part_heads):
                     at = slice(i * HD, (i + 1) * HD)
                     head = s * part_heads + i
-                    mine = own[slot, s, d, :, at]
-                    merged = mine + across(factors[d][0], head) * (precv[slot, s, d, :, at].astype(F32) - mine)
+                    mine = own[slot, s, side[d], :, at]
+                    merged = mine + across(factors[d][0], head) * (precv[slot, s, side[d], :, at].astype(F32) - mine)
                     merged = merged + across(factors[d][1], head) * (rs[d, k + 1, s, :, at].astype(F32) - mine)
                     rsd[d, k, s, :, at] = merged.astype(BF16)
 
-                if d == 0:
+                @pl.when(k < (far if carries else far - 1))
+                def _():
+                    part_copy(d, k, s).wait_send()
+
+                if carries:
+                    part_copy(d, k, s).start()
+                else:
 
                     @pl.when(k < far)
                     def _():
-                        part_copy(0, k, s).wait_send()
-
-                    part_copy(0, k, s).start()
-                else:
-
-                    @pl.when(k < far - 1)
-                    def _():
-                        part_copy(1, k, s).wait_send()
-
-                    @pl.when(k < far)
-                    def _():
-                        part_copy(1, k, s).start()
+                        part_copy(d, k, s).start()
 
         for n in range(per_step):
             b = j * per_step + n
@@ -403,9 +463,24 @@
             def _():
                 home(b)
 
+    home_stats = jnp.zeros((half, HD), F32)
+    for head in range(heads):
+        tile = hl[pl.ds(head, rows, stride=heads), :]
+        home_stats = jnp.where(lane == head, tile[:half], home_stats)
+        home_stats = jnp.where(lane == head + heads, tile[half:], home_stats)
+    base, weights = shares([lown[far - 1, 1], lprecv[far - 1, 1], home_stats])
+    for s in range(PARTS):
+        for i in range(part_heads):
+            at = slice(i * HD, (i + 1) * HD)
+            head = s * part_heads + i
+            mine = own[far - 1, s, 1, :, at]
+            merged = mine + across(weights[0], head) * (precv[far - 1, s, 1, :, at].astype(F32) - mine)
+            merged = merged + across(weights[1], head) * (ho[pl.ds(head, rows, stride=heads), :] - mine)
+            own[far - 1, s, 1, :, at] = merged
+
     for d in (0, 1):
         stat_copy(d, 1).wait_recv()
-    total, weights = shares([lown[far - 1, 1], lprecv[far - 1, 1], rss[0, 1], rss[1, 1]])
+    total, weights = shares([base, rss[0, 1], rss[1, 1]])
     for s in range(PARTS):
         for d in (0, 1):
             part_copy(d, 1, s).wait_recv()
@@ -413,13 +488,8 @@
             at = slice(i * HD, (i + 1) * HD)
             head = s * part_heads + i
             mine = own[far - 1, s, 1, :, at]
-            merged = mine + across(weights[0], head) * (precv[far - 1, s, 1, :, at].astype(F32) - mine)
-            merged = merged + across(weights[1], head) * (rs[0, 1, s, :, at].astype(F32) - mine)
-            merged = merged + across(weights[2], head) * (rs[1, 1, s, :, at].astype(F32) - mine)
-            home_lse = hl[pl.ds(head, rows, stride=heads), :]
-            home_out = ho[pl.ds(head, rows, stride=heads), :]
-            share = 1.0 / (1.0 + jnp.exp2(across(total, head) - home_lse))
-            merged = merged + share * (home_out - merged)
+            merged = mine + across(weights[0], head) * (rs[0, 1, s, :, at].astype(F32) - mine)
+            merged = merged + across(weights[1], head) * (rs[1, 1, s, :, at].astype(F32) - mine)
             out_ref[:, s * width + i * HD : s * width + (i + 1) * HD] = merged.astype(BF16)
 
     for d in (0, 1):
@@ -451,21 +521,13 @@
     slots = suffix_keys.shape[1]
     half = rows // 2
 
-    ids = lax.axis_index("seq") * pages + jnp.arange(pages, dtype=jnp.int32)
-    held = jnp.any(page_table[:, :, None] == ids[None, None, :], axis=1)
-    penalty = jnp.where(held, 0.0, LOW).astype(BF16)
-    penalty = jnp.repeat(penalty, page, axis=1)
-    penalty = jnp.concatenate([penalty, jnp.zeros((HD - NPREF, tokens), BF16)], axis=0)
-    onehot = (prefix_id[:, None] == jnp.arange(HD, dtype=jnp.int32)[None, :]).astype(BF16)
-    onehot = onehot.reshape(devices, rows, HD)
-
     any_space = pl.BlockSpec(memory_space=pl.ANY)
     vmem = pl.BlockSpec(memory_space=pltpu.VMEM)
     smem = pl.BlockSpec(memory_space=pltpu.SMEM)
     dma = pltpu.SemaphoreType.DMA
     chunk = (PARTS, 2, rows, width)
     return pl.pallas_call(
-        functools.partial(kernel, chips, math.log2(math.e) / math.sqrt(HD)),
+        functools.partial(kernel, chips, math.log2(math.e) / math.sqrt(HD), page),
         out_shape=jax.ShapeDtypeStruct((rows, columns), BF16),
         in_specs=[any_space, vmem, vmem, any_space, any_space, smem, any_space, any_space, vmem, vmem],
         out_specs=vmem,
@@ -475,6 +537,10 @@
             pltpu.VMEM((tokens, kv_columns), BF16),
             pltpu.VMEM((tokens, kv_columns), BF16),
             pltpu.VMEM((KV, 2 * HD, tokens), BF16),
+            pltpu.VMEM((devices * rows, HD), BF16),
+            pltpu.VMEM((KV // PARTS, 4 * (heads // KV) * rows, tokens), F32),
+            pltpu.VMEM((KV // PARTS, 4 * (heads // KV) * rows, tokens), F32),
+            pltpu.VMEM((KV // PARTS, 4 * (heads // KV) * rows, tokens), BF16),
             pltpu.VMEM((KV, tokens, 2 * HD), BF16),
             pltpu.VMEM((rows, slots, kv_columns), BF16),
             pltpu.VMEM((rows, slots, kv_columns), BF16),
@@ -520,8 +586,8 @@
         suffix_lens,
         prefix_keys.reshape(tokens, kv_columns),
         prefix_values.reshape(tokens, kv_columns),
-        penalty,
-        onehot,
+        page_table,
+        prefix_id.reshape(-1, HD),
     )
 
 

time: 100 us -> 89.7 us (0.90); the launches traced: 99.9 us -> 88.4 us
  Pallas kernels: 94.9 us -> 86.8 us
  other arithmetic: 1.72 us -> 0 us
  local copies, waits for them, and re-layouts: 3.23 us -> 1.57 us
    pallas_call x1, Pallas kernels: 94.9 us -> 86.8 us  [local(): pl.pallas_call(functools.partial(kernel, chips, math.log2(math.e) / math....]
where the time goes in v2:
time: 89.7 us; the launch traced here: 88.4 us
  Pallas kernels  86.8 us (97%)
  local copies, waits for them, and re-layouts  1.57 us (2%)
    pallas_call x1, Pallas kernels, local(): pl.pallas_call(functools.partial(kernel, chips, math.log2(math.e) / math....  86.8 us

profile of v2, /device:TPU:70, one launch (start us, length us, event | category | flops | bytes accessed | tf_op | source)
XLA Modules:
  0.0 88.4 jit_solution(2845608386834700762)
XLA Ops:
  0.0 86.8 %shard_map.100 = bf16[16,4096]{1,0:T(8,128)(2,1)} custom-call(bf16[16,4096]{1,0:T(8,128)(2,1)} %q_hbm.1, bf16[16,1024]{1,0:T(8,128)(2,1)} %nk_ref.1, bf16[16,1024]{1,0:T(8,128)(2,1)} %nv_ref.1, bf16[16,256,1024]{2,1,0:T(8,128)(2,1)} %ks_hbm.1, bf16[16,256,1024]{2,1,0:T(8,128)(2,1)} %vs_hbm.1, s32[16]{0:T(128)} %lens_ref.1, bf16[1024,1024]{1,0:T(8,128)(2,1)} %bitcast.3, ...), custom_call_target="tpu_custom_call" | custom-call | tf_op jit(solution)/shard_map/pallas_call | solution.py:529
  86.8 1.6 %copy.12 = bf16[16,4096]{1,0:T(8,128)(2,1)} copy(bf16[16,4096]{1,0:T(8,128)(2,1)} %shard_map.100) | data formatting | bytes 262144
